TPU v7x, 32 devices: a whole 2x2x4 slice. The times are simulated.
32 devices in a mesh: groups: 2 (over y), blk: 16 (over z, x, core).
Axes of the slice: x: 2, y: 2, z: 4, core: 2. Of those that a mesh axis runs over, the one named last changes fastest.
Arguments:
- current_states: float32 [16, 8192], P(None, ('groups', 'blk')), parts along dimension 1, may hold values from -0.5 to 0.5
- next_states: float32 [16, 8192], P(None, ('groups', 'blk')), parts along dimension 1, may hold values from -1 to 1
- next_values: float32 [8192], P(('groups', 'blk')), parts along dimension 0, may hold values from 0 to 2.5
- vol_table: float32 [12, 16], replicated, may hold values from 0.15 to 0.45
- date_index: int32 [1], replicated, may hold values from 0 to 11
- strike: float32 [1], replicated, may hold values from 0.8 to 1.2
Outputs:
- continuation: float32 [8192], P(('groups', 'blk')), parts along dimension 0
- node_value: float32 [8192], P(('groups', 'blk')), parts along dimension 0
There are 2 independent parts, one for each index of `groups`. A program takes and returns all parts, laid end to end along the dimension named above; an argument that names none is the same for every part. Nothing has to cross between parts.
All inputs are finite; a program needn't handle non-finite values.
Results may differ from a plain program's by a relative error of at most 0.00012.
Values sent between devices are 32-bit elements; how exact they have to be, the bound alone decides.
No kernel may reach another device: no remote copies, remote signals or barrier semaphores. Data moves between devices by JAX's collectives and lax.ppermute only.
A program may use at most 64 MiB of HBM per device.

v0:
```python
import functools
import math

import jax
import jax.numpy as jnp
from jax import lax
from jax.experimental import pallas as pl
from jax.experimental.pallas import tpu as pltpu
from jax.sharding import PartitionSpec as P


rate_year = 0.05
step_years = 0.1
log2_e = math.log2(math.e)
lanes = 128
lane_tile = 512
row_tile = 1024
depth = 128
vmem_grant = 16 * 1024 * 1024 + 4096


def scaled_states(current_states, next_states, vol_table, date_index):
    date_count = vol_table.shape[0]
    picked = (jnp.arange(date_count, dtype=jnp.int32) == date_index[0]).astype(jnp.float32)
    vol_row = jnp.sum(vol_table * picked[:, None], axis=0)
    spread = vol_row * math.sqrt(step_years)
    drift_term = (rate_year - 0.5 * vol_row * vol_row) * step_years
    anchor = (current_states + drift_term[:, None]) / spread[:, None]
    target = next_states / spread[:, None]
    anchor_half = 0.5 * jnp.sum(anchor * anchor, axis=0, keepdims=True)
    target_half = 0.5 * jnp.sum(target * target, axis=0, keepdims=True)
    return (anchor, anchor_half, target, target_half)


def kernel_block(source_states, source_norms, sink_states, sink_norms):
    inner_term = lax.dot_general(
        source_states,
        sink_states,
        (((0,), (0,)), ((), ())),
        precision=lax.Precision.HIGHEST,
        preferred_element_type=jnp.float32,
    )
    return jnp.exp(inner_term - source_norms.reshape(-1, 1) - sink_norms)


def block_rows(row_count):
    if row_count <= 4096:
        return row_count
    return math.gcd(row_count, 4096)


def finish(current_states, totals, strike):
    continuation = math.exp(-rate_year * step_years) * totals[0] / totals[1]
    payoff = jnp.maximum(jnp.max(jnp.exp(current_states), axis=0) - strike[0], 0.0)
    return (continuation, jnp.maximum(payoff, continuation))


def gathered_body(current_states, next_states, next_values, vol_table, date_index, strike):
    anchor, anchor_half, target, target_half = scaled_states(
        current_states, next_states, vol_table, date_index
    )
    local_count = anchor.shape[1]
    pieces = (
        lax.all_gather(anchor, "blk", axis=1, tiled=True),
        lax.all_gather(anchor_half, "blk", axis=1, tiled=True),
    )
    row_count = pieces[0].shape[1]
    block_size = block_rows(row_count)

    def density_block(number, inner_sum):
        source_part = lax.dynamic_slice_in_dim(pieces[0], number * block_size, block_size, 1)
        norm_part = lax.dynamic_slice_in_dim(pieces[1], number * block_size, block_size, 1)
        return inner_sum + jnp.sum(
            kernel_block(source_part, norm_part, target, target_half), axis=0
        )

    density = lax.fori_loop(
        0, row_count // block_size, density_block, jnp.zeros((local_count,), jnp.float32)
    )
    extras = jnp.concatenate(
        [target_half, (next_values / density)[None, :], (1.0 / density)[None, :]], axis=0
    )
    add_pieces = (
        lax.all_gather(target, "blk", axis=1, tiled=True),
        lax.all_gather(extras, "blk", axis=1, tiled=True),
    )

    def weighted_block(number, inner_sum):
        sink_part = lax.dynamic_slice_in_dim(add_pieces[0], number * block_size, block_size, 1)
        extra_part = lax.dynamic_slice_in_dim(add_pieces[1], number * block_size, block_size, 1)
        weights = kernel_block(sink_part, extra_part[0:1], anchor, anchor_half)
        return inner_sum + jnp.dot(
            extra_part[1:3],
            weights,
            precision=lax.Precision.HIGHEST,
            preferred_element_type=jnp.float32,
        )

    totals = lax.fori_loop(
        0, row_count // block_size, weighted_block, jnp.zeros((2, local_count), jnp.float32)
    )
    return finish(current_states, totals, strike)


def in_three(x):
    first = x.astype(jnp.bfloat16)
    rest = x - first.astype(jnp.float32)
    second = rest.astype(jnp.bfloat16)
    third = (rest - second.astype(jnp.float32)).astype(jnp.bfloat16)
    return first, second, third


def with_norm(pieces, norm, shift):
    rows = lax.broadcasted_iota(jnp.int32, (16, norm.shape[1]), 0)
    tile = jnp.where((rows >= 3 - shift) & (rows < 6 - shift), 1.0, 0.0)
    for k, part in enumerate(in_three(norm)):
        tile = jnp.where(rows == k + shift, part.astype(jnp.float32), tile)
    stacked = list(pieces) + [tile.astype(jnp.bfloat16)]
    height = sum(piece.shape[0] for piece in stacked)
    stacked.append(jnp.zeros((depth - height, norm.shape[1]), jnp.bfloat16))
    return jnp.concatenate(stacked, axis=0)


def source_operand(states, inverse, drift_term):
    anchor = (states + drift_term) * inverse
    half = (0.5 * log2_e) * jnp.sum(anchor * anchor, axis=0, keepdims=True)
    a1, a2, a3 = in_three(anchor * log2_e)
    return with_norm((a1, a1, a2, a1, a2, a3), -half, 0).T


def sink_operand(states, inverse):
    target = states * inverse
    half = (0.5 * log2_e) * jnp.sum(target * target, axis=0, keepdims=True)
    t1, t2, t3 = in_three(target)
    return with_norm((t1, t2, t1, t3, t2, t1), -half, 3)


def build_sources(states_refs, columns_ref, left_ref):
    inverse, drift_term = columns_ref[0], columns_ref[1]
    assets = inverse.shape[0]
    slabs = left_ref.shape[0] // lanes // len(states_refs)
    for slab in range(left_ref.shape[0] // lanes):
        row = slab % slabs * assets
        states = states_refs[slab // slabs][row : row + assets, :]
        left_ref[slab * lanes : (slab + 1) * lanes, :] = source_operand(states, inverse, drift_term)


def build_sinks(states_refs, start, columns_ref, right_ref):
    inverse = columns_ref[0]
    assets = inverse.shape[0]
    slabs = right_ref.shape[1] // lanes // len(states_refs)
    for slab in range(right_ref.shape[1] // lanes):
        row = start + slab % slabs * assets
        states = states_refs[slab // slabs][row : row + assets, :]
        right_ref[:, slab * lanes : (slab + 1) * lanes] = sink_operand(states, inverse)


def add_density(left_refs, right_ref, density_ref, first_row, base_ref=None, base_row=0):
    width = math.gcd(right_ref.shape[1], lane_tile)
    for number in range(right_ref.shape[1] // width):
        right = right_ref[:, number * width : (number + 1) * width]
        total = jnp.zeros((8, width), jnp.float32)
        for left_ref in left_refs:
            height = math.gcd(left_ref.shape[0], row_tile)
            for k in range(left_ref.shape[0] // height):
                exponent = jnp.dot(
                    left_ref[k * height : (k + 1) * height, :],
                    right,
                    preferred_element_type=jnp.float32,
                )
                total += jnp.sum(jnp.exp2(exponent).reshape(height // 8, 8, width), axis=0)
        sums = jnp.sum(total, axis=0, keepdims=True)
        for slab in range(width // lanes):
            row = number * (width // lanes) + slab
            value = sums[:, slab * lanes : (slab + 1) * lanes]
            if base_ref is not None:
                value += base_ref[base_row + row : base_row + row + 1, :]
            density_ref[first_row + row : first_row + row + 1, :] = value


def pack_kernel(*refs):
    row = 0
    for ref in refs[:-1]:
        height = min(ref.shape[0], refs[-1].shape[0] - row)
        refs[-1][row : row + height, :] = ref[0:height, :]
        row += height


def columns_kernel(table_ref, packed_ref, columns_ref):
    dates, assets = table_ref.shape[0] - 1, table_ref.shape[1]
    index = table_ref[dates : dates + 1, 0:1]
    rows = lax.broadcasted_iota(jnp.int32, (dates, assets), 0).astype(jnp.float32)
    vol_row = jnp.sum(
        jnp.where(rows == index, table_ref[0:dates, :], 0.0), axis=0, keepdims=True
    )
    square = (assets, assets)
    diagonal = lax.broadcasted_iota(jnp.int32, square, 0) == lax.broadcasted_iota(
        jnp.int32, square, 1
    )
    vol = jnp.sum(
        jnp.where(diagonal, jnp.broadcast_to(vol_row, square), 0.0), axis=1, keepdims=True
    )
    vol = jnp.broadcast_to(vol, (assets, lanes))
    columns_ref[0] = 1.0 / (vol * math.sqrt(step_years))
    columns_ref[1] = (rate_year - 0.5 * vol * vol) * step_years


def payoff_kernel(table_ref, packed_ref, payoff_ref):
    assets = table_ref.shape[1]
    strike = table_ref[table_ref.shape[0] - 1 :, 1:2]
    for slab in range(payoff_ref.shape[0]):
        prices = jnp.exp(packed_ref[slab * assets : (slab + 1) * assets, :])
        best = jnp.max(prices, axis=0, keepdims=True)
        payoff_ref[slab : slab + 1, :] = jnp.maximum(best - strike, 0.0)


def near_kernel(sources, columns_ref, first_ref, second_ref, left_ref, right_ref, density_ref):
    build_sources((first_ref, second_ref), columns_ref, left_ref)
    build_sinks((first_ref, second_ref), sources, columns_ref, right_ref)
    add_density((left_ref,), right_ref, density_ref, 0)


def near_other_kernel(columns_ref, other_ref, left_ref, right_ref, density_ref):
    build_sinks((other_ref,), 0, columns_ref, right_ref)
    add_density((left_ref,), right_ref, density_ref, 0)


def mid_kernel(sources, columns_ref, mid_ref, near_left, near_right, base, left, right, density):
    build_sinks((mid_ref,), sources, columns_ref, right)
    build_sources((mid_ref,), columns_ref, left)
    add_density((near_left, left), right, density, base.shape[0])
    add_density((left,), near_right, density, 0, base)


def far_kernel(
    sources,
    columns_ref,
    far_ref,
    near_left,
    mid_left,
    near_right,
    mid_right,
    base,
    left,
    right,
    density,
):
    near_slabs = near_right.shape[1] // lanes
    build_sinks((far_ref,), sources, columns_ref, right)
    build_sources((far_ref,), columns_ref, left)
    add_density((near_left, mid_left, left), right, density, base.shape[0])
    add_density((left,), near_right, density, 0, base)
    add_density((left,), mid_right, density, near_slabs, base, near_slabs)


def far_other_kernel(
    columns_ref,
    other_ref,
    near_left,
    mid_left,
    far_left,
    near_right,
    base,
    right,
    density,
):
    add_density((mid_left, far_left), near_right, density, 0, base)
    build_sinks((other_ref,), 0, columns_ref, right)
    add_density((near_left, mid_left, far_left), right, density, base.shape[0])


def matrix_kernel(left_ref, *refs):
    matrix_ref = refs[-1]
    place = 0
    for right_ref in refs[:-1]:
        width = math.gcd(right_ref.shape[1], lane_tile)
        for number in range(right_ref.shape[1] // width):
            matrix_ref[:, place : place + width] = jnp.exp2(
                jnp.dot(
                    left_ref[...],
                    right_ref[:, number * width : (number + 1) * width],
                    preferred_element_type=jnp.float32,
                )
            )
            place += width


def weight_kernel(assets, matrix_ref, density_ref, received_ref, *refs):
    *values_refs, payoff_ref, continuation_ref, node_ref, ratio_ref = refs
    slabs = density_ref.shape[0]
    half = slabs // 2
    inverse = 1.0 / jnp.concatenate(
        [
            density_ref[:half, :] + received_ref[half:, :],
            density_ref[half:, :] + received_ref[:half, :],
        ],
        axis=0,
    )
    ratio_ref[1] = inverse
    row = 0
    for k, values_ref in enumerate(values_refs):
        rows_per_slab = 2 * assets + 1 if k < 4 else assets + 1
        count = values_ref.shape[0] // rows_per_slab
        values = values_ref[values_ref.shape[0] - count :, :]
        ratio_ref[0, row : row + count, :] = values * inverse[row : row + count]
        row += count
    count = matrix_ref.shape[0]
    height = math.gcd(count, 64)
    sums = []
    for k in range(count // height):
        weighted = jnp.zeros((height, lanes), jnp.float32)
        mass = jnp.zeros((height, lanes), jnp.float32)
        for slab in range(slabs):
            piece = matrix_ref[k * height : (k + 1) * height, slab * lanes : (slab + 1) * lanes]
            weighted += piece * ratio_ref[0, slab : slab + 1, :]
            mass += piece * ratio_ref[1, slab : slab + 1, :]
        sums.append((weighted, mass))
    per_slab = lanes // height
    for slab in range(count // lanes):
        group = sums[slab * per_slab : (slab + 1) * per_slab]
        weighted, mass = (
            jnp.sum(jnp.concatenate([pair[k] for pair in group], axis=0).T, axis=0, keepdims=True)
            for k in range(2)
        )
        continuation = math.exp(-rate_year * step_years) * weighted / mass
        continuation_ref[slab : slab + 1, :] = continuation
        node_ref[slab : slab + 1, :] = jnp.maximum(payoff_ref[slab : slab + 1, :], continuation)


vmem = pl.BlockSpec(memory_space=pltpu.VMEM)


def local_call(kernel, in_specs, out_shapes, matmul_pairs=0, scratch_shapes=()):
    cost = pl.CostEstimate(
        flops=2 * depth * matmul_pairs, transcendentals=matmul_pairs, bytes_accessed=0
    )
    return pl.pallas_call(
        kernel,
        out_shape=out_shapes,
        in_specs=in_specs,
        out_specs=[vmem] * len(out_shapes),
        scratch_shapes=scratch_shapes,
        cost_estimate=cost,
        compiler_params=pltpu.CompilerParams(vmem_limit_bytes=vmem_grant),
    )


def doubled_body(blk_size, current_states, next_states, next_values, vol_table, date_index, strike):
    assets, count = current_states.shape
    own_slabs = count // lanes

    def across(array, mask):
        return lax.ppermute(array, "blk", [(i, i ^ mask) for i in range(blk_size)])

    def floats(*shape):
        return jax.ShapeDtypeStruct(shape, jnp.float32)

    def halves(*shape):
        return jax.ShapeDtypeStruct(shape, jnp.bfloat16)

    pieces = [
        part[:, slab * lanes : (slab + 1) * lanes]
        for part in (current_states, next_states)
        for slab in range(own_slabs)
    ]
    rows = lax.pad(
        next_values.reshape(own_slabs, lanes), jnp.float32(0), ((0, assets - own_slabs, 0), (0, 0, 0))
    )
    tile_rows = lax.broadcasted_iota(jnp.int32, rows.shape, 0)
    pieces.append(jnp.where(tile_rows < own_slabs, rows, pieces[0]))
    (packed,) = local_call(
        pack_kernel, [vmem] * len(pieces), [floats((2 * assets + 1) * own_slabs, lanes)]
    )(*pieces)
    places = lax.broadcasted_iota(jnp.int32, (1, assets), 1)
    last = jnp.where(places == 0, date_index.astype(jnp.float32), jnp.where(places == 1, strike, 0.0))
    table = jnp.concatenate([vol_table, last], axis=0)
    (columns,) = local_call(columns_kernel, [vmem, vmem], [floats(2, assets, lanes)])(table, packed)

    slabs = own_slabs
    mask = blk_size // 2
    while mask > 4:
        received = across(packed, mask)
        cuts = (0, assets * slabs, 2 * assets * slabs, (2 * assets + 1) * slabs)
        packed = jnp.concatenate(
            [part[a:b] for a, b in zip(cuts, cuts[1:]) for part in (packed, received)], axis=0
        )
        if slabs == own_slabs:
            packed, columns = lax.optimization_barrier((packed, columns))
        slabs *= 2
        mask //= 2
    sources = assets * slabs
    near = across(packed, 4)
    mid = across(packed, 6)
    far = across(packed, 2)
    (payoff,) = local_call(payoff_kernel, [vmem, vmem], [floats(own_slabs, lanes)])(table, packed)
    nodes = slabs * lanes
    targets, values = slice(sources, 2 * sources), slice(2 * sources, None)

    def sinks(first, second):
        return jnp.concatenate([first[targets], second[targets], first[values], second[values]])

    near_other = across(sinks(packed, near), 1)
    left, right, base = local_call(
        functools.partial(near_kernel, sources),
        [vmem] * 3,
        [halves(2 * nodes, depth), halves(depth, 2 * nodes), floats(2 * slabs, lanes)],
        4 * nodes * nodes,
    )(columns, packed, near)
    other_right, other_base = local_call(
        near_other_kernel,
        [vmem] * 3,
        [halves(depth, 2 * nodes), floats(2 * slabs, lanes)],
        4 * nodes * nodes,
    )(columns, near_other, left)
    mid_left, mid_right, mid_base = local_call(
        functools.partial(mid_kernel, sources),
        [vmem] * 5,
        [halves(nodes, depth), halves(depth, nodes), floats(3 * slabs, lanes)],
        5 * nodes * nodes,
    )(columns, mid, left, right, base)
    far_other = across(sinks(mid, far), 1)
    far_left, far_right, density = local_call(
        functools.partial(far_kernel, sources),
        [vmem] * 7,
        [halves(nodes, depth), halves(depth, nodes), floats(4 * slabs, lanes)],
        7 * nodes * nodes,
    )(columns, far, left, mid_left, right, mid_right, mid_base)
    far_other_right, other_density = local_call(
        far_other_kernel,
        [vmem] * 7,
        [halves(depth, 2 * nodes), floats(4 * slabs, lanes)],
        12 * nodes * nodes,
    )(columns, far_other, left, mid_left, far_left, other_right, other_base)
    density = jnp.concatenate([density, other_density], axis=0)
    received = across(density, 1)
    (matrix,) = local_call(
        matrix_kernel, [vmem] * 6, [floats(count, 8 * nodes)], 8 * count * nodes
    )(left[:count], right, mid_right, far_right, other_right, far_other_right)
    continuation, node_value = local_call(
        functools.partial(weight_kernel, assets),
        [vmem] * 10,
        [floats(own_slabs, lanes)] * 2,
        scratch_shapes=[pltpu.VMEM((2, 8 * slabs, lanes), jnp.float32)],
    )(
        matrix,
        density,
        received,
        packed,
        near,
        mid,
        far,
        near_other,
        far_other,
        payoff,
    )
    return continuation.reshape(count), node_value.reshape(count)


def solution(mesh):
    blk_size = mesh.shape["blk"]
    placed = (
        P(None, ("groups", "blk")),
        P(None, ("groups", "blk")),
        P(("groups", "blk")),
        P(),
        P(),
        P(),
    )
    doubled = blk_size in (16, 32)
    return jax.shard_map(
        functools.partial(doubled_body, blk_size) if doubled else gathered_body,
        mesh=mesh,
        in_specs=placed,
        out_specs=(P(("groups", "blk")), P(("groups", "blk"))),
        check_vma=False,
    )
```

profile of v0, /device:TPU:0, one launch (start us, length us, event | category | flops | bytes accessed | tf_op | source)
XLA Modules:
  0.0 23.7 jit_solution(13684258337071764463)
XLA Ops:
  0.6 0.8 %pad_select_fusion = (f32[16,128]{1,0:T(8,128)S(1)}, f32[16,128]{1,0:T(8,128)S(1)}, f32[16,128]{1,0:T(8,128)S(1)}, f32[16,128]{1,0:T(8,128)S(1)}, f32[16,128]{1,0:T(8,128)S(1)}) fusion(f32[2,128]{1,0:T(2,128)} %bitcast.6, pred[16]{0:T(512)(128)(4,1)S(1)} %iota_compare_fusion, f32[16,256]{1,0:T(8,128)} %param.6, f32[16,256]{1,0:T(8,128)} %param.7), kind=kLoop, calls=%fused_computation.3 | loop fusion | flops 2048 | bytes 74768 | tf_op jit(solution)/shard_map/jit(_where)/select_n | solution.py:370
  1.5 4.1 %collective-permute-start = (f32[66,128]{1,0:T(8,128)S(1)}, f32[66,128]{1,0:T(8,128)S(1)}, u32[]{:S(2)}, u32[]{:S(2)}) collective-permute-start(f32[66,128]{1,0:T(8,128)S(1)} %shard_map.77.packed_ref), channel_id=1, source_target_pairs={{0,8},{1,9},{2,10},{3,11},{4,12},{5,13},{6,14},{7,15},{8,0},{9,1},... | collective-permute-start | bytes 101384 | tf_op jit(solution)/shard_map/ppermute | solution.py:353
  6.9 0.7 %pad_maximum_fusion.2.table_ref = f32[13,16]{1,0:T(8,128)S(1)} fusion(f32[1,16]{1,0:T(1,128)S(1)} %compare_select_fusion.1, f32[12,16]{1,0:T(8,128)} %param.9), kind=kLoop, calls=%fused_computation.2 | loop fusion | flops 208 | bytes 1664 | tf_op jit(solution)/shard_map/concatenate | solution.py:376
  7.6 0.1 shard_map.78.columns_ref
  7.8 0.2 collective-permute-done
  8.0 1.6 %collective-permute-start.1 = (f32[132,128]{1,0:T(8,128)S(1)}, f32[132,128]{1,0:T(8,128)S(1)}, u32[]{:S(2)}, u32[]{:S(2)}) collective-permute-start(f32[132,128]{1,0:T(8,128)S(1)} %concatenate.15.first_ref.packed_ref.refs_0_), channel_id=1, source_target_pairs={{0,4},{1,5},{2,6},{3,7},{4,0},{5,1},{6,2},{7,3},{8,12},{9,13},{10,... | collective-permute-start | bytes 202760 | tf_op jit(solution)/shard_map/ppermute | solution.py:353
  9.6 1.6 %collective-permute-start.2 = (f32[132,128]{1,0:T(8,128)S(1)}, f32[132,128]{1,0:T(8,128)S(1)}, u32[]{:S(2)}, u32[]{:S(2)}) collective-permute-start(f32[132,128]{1,0:T(8,128)S(1)} %concatenate.15.first_ref.packed_ref.refs_0_), channel_id=1, source_target_pairs={{0,6},{1,7},{2,4},{3,5},{4,2},{5,3},{6,0},{7,1},{8,14},{9,15},{10,... | collective-permute-start | bytes 202760 | tf_op jit(solution)/shard_map/ppermute | solution.py:353
  11.2 0.3 %collective-permute-start.3 = (f32[132,128]{1,0:T(8,128)S(1)}, f32[132,128]{1,0:T(8,128)S(1)}, u32[]{:S(2)}, u32[]{:S(2)}) collective-permute-start(f32[132,128]{1,0:T(8,128)S(1)} %concatenate.15.first_ref.packed_ref.refs_0_), channel_id=1, source_target_pairs={{0,2},{1,3},{2,0},{3,1},{4,6},{5,7},{6,4},{7,5},{8,10},{9,11},{10,... | collective-permute-start | bytes 202760 | tf_op jit(solution)/shard_map/ppermute | solution.py:353
  11.5 0.1 shard_map.85.refs_6_
  11.6 0.8 %collective-permute-done.1.second_ref.refs_1_ = f32[132,128]{1,0:T(8,128)S(1)} collective-permute-done((f32[132,128]{1,0:T(8,128)S(1)}, f32[132,128]{1,0:T(8,128)S(1)}, u32[]{:S(2)}, u32[]{:S(2)}) %collective-permute-start.1) | collective-permute-done | bytes 67616 | tf_op jit(solution)/shard_map/ppermute | solution.py:353
  12.5 0.1 collective-permute-start.4
  12.5 2.2 %collective-permute-done.2.mid_ref.refs_2_ = f32[132,128]{1,0:T(8,128)S(1)} collective-permute-done((f32[132,128]{1,0:T(8,128)S(1)}, f32[132,128]{1,0:T(8,128)S(1)}, u32[]{:S(2)}, u32[]{:S(2)}) %collective-permute-start.2) | collective-permute-done | bytes 67616 | tf_op jit(solution)/shard_map/ppermute | solution.py:353
  14.8 0.7 %collective-permute-done.3.far_ref.refs_3_ = f32[132,128]{1,0:T(8,128)S(1)} collective-permute-done((f32[132,128]{1,0:T(8,128)S(1)}, f32[132,128]{1,0:T(8,128)S(1)}, u32[]{:S(2)}, u32[]{:S(2)}) %collective-permute-start.3) | collective-permute-done | bytes 67616 | tf_op jit(solution)/shard_map/ppermute | solution.py:353
  15.5 0.1 collective-permute-start.5
  15.6 0.8 %shard_map.79 = (bf16[1024,128]{1,0:T(8,128)(2,1)S(1)}, bf16[128,1024]{1,0:T(8,128)(2,1)S(1)}, f32[8,128]{1,0:T(8,128)S(1)}) custom-call(f32[2,16,128]{2,1,0:T(8,128)S(1)} %shard_map.78.columns_ref, f32[132,128]{1,0:T(8,128)S(1)} %concatenate.15.first_ref.packed_ref.refs_0_, f32[132,128]{1,0:T(8,128)S(1)} %collective-permute-done.1.second_ref.refs_1_), custom_call_target="tpu_custom_call" | custom-call | flops 268435456 | tf_op jit(solution)/shard_map/pallas_call | solution.py:403
  16.4 0.9 %shard_map.80 = (bf16[512,128]{1,0:T(8,128)(2,1)S(1)}, bf16[128,512]{1,0:T(8,128)(2,1)S(1)}, f32[12,128]{1,0:T(8,128)S(1)}) custom-call(f32[2,16,128]{2,1,0:T(8,128)S(1)} %shard_map.78.columns_ref, f32[132,128]{1,0:T(8,128)S(1)} %collective-permute-done.2.mid_ref.refs_2_, bf16[1024,128]{1,0:T(8,128)(2,1)S(1)} %get-tuple-element.21.near_left.left_ref, ...), custom_call_target="tpu_custom_call" | custom-call | flops 335544320 | tf_op jit(solution)/shard_map/pallas_call | solution.py:415
  17.3 1.1 %shard_map.81 = (bf16[512,128]{1,0:T(8,128)(2,1)S(1)}, bf16[128,512]{1,0:T(8,128)(2,1)S(1)}, f32[16,128]{1,0:T(8,128)S(1)}) custom-call(f32[2,16,128]{2,1,0:T(8,128)S(1)} %shard_map.78.columns_ref, f32[132,128]{1,0:T(8,128)S(1)} %collective-permute-done.3.far_ref.refs_3_, bf16[1024,128]{1,0:T(8,128)(2,1)S(1)} %get-tuple-element.21.near_left.left_ref, ...), custom_call_target="tpu_custom_call" | custom-call | flops 469762048 | tf_op jit(solution)/shard_map/pallas_call | solution.py:422
  18.5 0.0 collective-permute-done.4.other_ref.refs_4_
  18.5 0.7 %shard_map.82 = (bf16[128,1024]{1,0:T(8,128)(2,1)S(1)}, f32[8,128]{1,0:T(8,128)S(1)}) custom-call(f32[2,16,128]{2,1,0:T(8,128)S(1)} %shard_map.78.columns_ref, f32[136,128]{1,0:T(8,128)S(1)} %collective-permute-done.4.other_ref.refs_4_, bf16[1024,128]{1,0:T(8,128)(2,1)S(1)} %get-tuple-element.21.near_left.left_ref), custom_call_target="tpu_custom_call" | custom-call | flops 268435456 | tf_op jit(solution)/shard_map/pallas_call | solution.py:409
  19.2 0.0 collective-permute-done.5.other_ref.refs_5_
  19.2 1.8 %shard_map.83 = (bf16[128,1024]{1,0:T(8,128)(2,1)S(1)}, f32[16,128]{1,0:T(8,128)S(1)}) custom-call(f32[2,16,128]{2,1,0:T(8,128)S(1)} %shard_map.78.columns_ref, f32[136,128]{1,0:T(8,128)S(1)} %collective-permute-done.5.other_ref.refs_5_, bf16[1024,128]{1,0:T(8,128)(2,1)S(1)} %get-tuple-element.21.near_left.left_ref, ...), custom_call_target="tpu_custom_call" | custom-call | flops 805306368 | tf_op jit(solution)/shard_map/pallas_call | solution.py:428
  21.1 0.6 %collective-permute-start.6 = (f32[32,128]{1,0:T(8,128)S(1)}, f32[32,128]{1,0:T(8,128)S(1)}, u32[]{:S(2)}, u32[]{:S(2)}) collective-permute-start(f32[32,128]{1,0:T(8,128)S(1)} %constant_dynamic-update-slice_fusion.density_ref), channel_id=1, source_target_pairs={{0,1},{1,0},{2,3},{3,2},{4,5},{5,4},{6,7},{7,6},{8,9},{9,8},{10,11... | collective-permute-start | bytes 49160 | tf_op jit(solution)/shard_map/ppermute | solution.py:353
  21.6 0.7 %shard_map.84.matrix_ref = f32[256,4096]{1,0:T(8,128)S(1)} custom-call(bf16[256,128]{1,0:T(8,128)(2,1)S(1)} %slice.67.left_ref, bf16[128,1024]{1,0:T(8,128)(2,1)S(1)} %get-tuple-element.22.near_right.refs_0_, bf16[128,512]{1,0:T(8,128)(2,1)S(1)} %get-tuple-element.24.mid_right.refs_1_, bf16[128,512]{1,0:T(8,128)(2,1)S(1)} %get-tuple-element.27.refs_2_, ...), custom_call_target="tpu_custom_call" | custom-call | flops 268435456 | tf_op jit(solution)/shard_map/pallas_call | solution.py:436
  22.3 0.1 collective-permute-done.6.received_ref
  22.5 1.2 %shard_map.86 = (f32[2,128]{1,0:T(2,128)}, f32[2,128]{1,0:T(2,128)}) custom-call(f32[256,4096]{1,0:T(8,128)S(1)} %shard_map.84.matrix_ref, f32[32,128]{1,0:T(8,128)S(1)} %constant_dynamic-update-slice_fusion.density_ref, f32[32,128]{1,0:T(8,128)S(1)} %collective-permute-done.6.received_ref, f32[132,128]{1,0:T(8,128)S(1)} %concatenate.15.first_ref.packed_ref.refs_0_, ...), custom_call_target="tpu_custom_call" | custom-call | tf_op jit(solution)/shard_map/pallas_call | solution.py:439
  (21 shorter events, 0.1 us)
Async XLA Ops:
  1.5 6.5 %collective-permute-start = (f32[66,128]{1,0:T(8,128)S(1)}, f32[66,128]{1,0:T(8,128)S(1)}, u32[]{:S(2)}, u32[]{:S(2)}) collective-permute-start(f32[66,128]{1,0:T(8,128)S(1)} %shard_map.77.packed_ref), channel_id=1, source_target_pairs={{0,8},{1,9},{2,10},{3,11},{4,12},{5,13},{6,14},{7,15},{8,0},{9,1},... | collective-permute-start | bytes 101384 | tf_op jit(solution)/shard_map/ppermute | solution.py:353
  8.0 4.5 %collective-permute-start.1 = (f32[132,128]{1,0:T(8,128)S(1)}, f32[132,128]{1,0:T(8,128)S(1)}, u32[]{:S(2)}, u32[]{:S(2)}) collective-permute-start(f32[132,128]{1,0:T(8,128)S(1)} %concatenate.15.first_ref.packed_ref.refs_0_), channel_id=1, source_target_pairs={{0,4},{1,5},{2,6},{3,7},{4,0},{5,1},{6,2},{7,3},{8,12},{9,13},{10,... | collective-permute-start | bytes 202760 | tf_op jit(solution)/shard_map/ppermute | solution.py:353
  9.6 5.2 %collective-permute-start.2 = (f32[132,128]{1,0:T(8,128)S(1)}, f32[132,128]{1,0:T(8,128)S(1)}, u32[]{:S(2)}, u32[]{:S(2)}) collective-permute-start(f32[132,128]{1,0:T(8,128)S(1)} %concatenate.15.first_ref.packed_ref.refs_0_), channel_id=1, source_target_pairs={{0,6},{1,7},{2,4},{3,5},{4,2},{5,3},{6,0},{7,1},{8,14},{9,15},{10,... | collective-permute-start | bytes 202760 | tf_op jit(solution)/shard_map/ppermute | solution.py:353
  11.2 4.3 %collective-permute-start.3 = (f32[132,128]{1,0:T(8,128)S(1)}, f32[132,128]{1,0:T(8,128)S(1)}, u32[]{:S(2)}, u32[]{:S(2)}) collective-permute-start(f32[132,128]{1,0:T(8,128)S(1)} %concatenate.15.first_ref.packed_ref.refs_0_), channel_id=1, source_target_pairs={{0,2},{1,3},{2,0},{3,1},{4,6},{5,7},{6,4},{7,5},{8,10},{9,11},{10,... | collective-permute-start | bytes 202760 | tf_op jit(solution)/shard_map/ppermute | solution.py:353
  12.5 6.0 %collective-permute-start.4 = (f32[136,128]{1,0:T(8,128)S(1)}, f32[136,128]{1,0:T(8,128)S(1)}, u32[]{:S(2)}, u32[]{:S(2)}) collective-permute-start(f32[136,128]{1,0:T(8,128)S(1)} %pad_maximum_fusion), channel_id=1, source_target_pairs={{0,1},{1,0},{2,3},{3,2},{4,5},{5,4},{6,7},{7,6},{8,9},{9,8},{10,11... | collective-permute-start | bytes 208904 | tf_op jit(solution)/shard_map/ppermute | solution.py:353
  15.5 3.7 %collective-permute-start.5 = (f32[136,128]{1,0:T(8,128)S(1)}, f32[136,128]{1,0:T(8,128)S(1)}, u32[]{:S(2)}, u32[]{:S(2)}) collective-permute-start(f32[136,128]{1,0:T(8,128)S(1)} %pad_maximum_fusion.1), channel_id=1, source_target_pairs={{0,1},{1,0},{2,3},{3,2},{4,5},{5,4},{6,7},{7,6},{8,9},{9,8},{10,11... | collective-permute-start | bytes 208904 | tf_op jit(solution)/shard_map/ppermute | solution.py:353
  21.1 1.4 %collective-permute-start.6 = (f32[32,128]{1,0:T(8,128)S(1)}, f32[32,128]{1,0:T(8,128)S(1)}, u32[]{:S(2)}, u32[]{:S(2)}) collective-permute-start(f32[32,128]{1,0:T(8,128)S(1)} %constant_dynamic-update-slice_fusion.density_ref), channel_id=1, source_target_pairs={{0,1},{1,0},{2,3},{3,2},{4,5},{5,4},{6,7},{7,6},{8,9},{9,8},{10,11... | collective-permute-start | bytes 49160 | tf_op jit(solution)/shard_map/ppermute | solution.py:353
where the time goes:
time: 23.9 us; the launch traced here: 23.7 us
  starting transfers between devices  8.37 us (35%)
  Pallas kernels  7.47 us (31%)
  waiting for transfers between devices  4.13 us (17%)
  between operations  2.06 us (9%)
  other arithmetic  1.58 us (7%)
    ppermute x7, starting transfers between devices, across(): return lax.ppermute(array, 'blk', [(i, i ^ mask) for i in range(blk_size)])  8.37 us
    ppermute x7, waiting for transfers between devices, across(): return lax.ppermute(array, 'blk', [(i, i ^ mask) for i in range(blk_size)])  4.13 us
    pallas_call x1, Pallas kernels, doubled_body(): local_call(far_other_kernel, [vmem] * 7, [halves(depth, 2 * nodes), float...  1.81 us
    pallas_call x1, Pallas kernels, doubled_body(): local_call(functools.partial(weight_kernel, assets), [vmem] * 10, [floats...  1.23 us
    pallas_call x1, Pallas kernels, doubled_body(): local_call(functools.partial(far_kernel, sources), [vmem] * 7, [halves(no...  1.15 us
    pallas_call x1, Pallas kernels, doubled_body(): local_call(functools.partial(mid_kernel, sources), [vmem] * 5, [halves(no...  0.88 us
    select_n x1, other arithmetic, doubled_body(): pieces.append(jnp.where(tile_rows < own_slabs, rows, pieces[0]))  0.84 us
    pallas_call x1, Pallas kernels, doubled_body(): local_call(functools.partial(near_kernel, sources), [vmem] * 3, [halves(2...  0.78 us
  transfers between devices with their start and end apart: 7, of which 5 were waited for; matrix products, arithmetic and copies ran while one was open for 3% of the time, Pallas kernels for 19%

commit v1 on v0

--- a/solution.py
+++ b/solution.py
@@ -261,12 +261,15 @@
     far_left,
     near_right,
     base,
+    own_density,
     right,
     density,
 ):
-    add_density((mid_left, far_left), near_right, density, 0, base)
+    rows = own_density.shape[0]
+    density[0:rows, :] = own_density[...]
+    add_density((mid_left, far_left), near_right, density, rows, base)
     build_sinks((other_ref,), 0, columns_ref, right)
-    add_density((near_left, mid_left, far_left), right, density, base.shape[0])
+    add_density((near_left, mid_left, far_left), right, density, rows + base.shape[0])
 
 
 def matrix_kernel(left_ref, *refs):
@@ -425,13 +428,12 @@
         [halves(nodes, depth), halves(depth, nodes), floats(4 * slabs, lanes)],
         7 * nodes * nodes,
     )(columns, far, left, mid_left, right, mid_right, mid_base)
-    far_other_right, other_density = local_call(
+    far_other_right, density = local_call(
         far_other_kernel,
-        [vmem] * 7,
-        [halves(depth, 2 * nodes), floats(4 * slabs, lanes)],
+        [vmem] * 8,
+        [halves(depth, 2 * nodes), floats(8 * slabs, lanes)],
         12 * nodes * nodes,
-    )(columns, far_other, left, mid_left, far_left, other_right, other_base)
-    density = jnp.concatenate([density, other_density], axis=0)
+    )(columns, far_other, left, mid_left, far_left, other_right, other_base, density)
     received = across(density, 1)
     (matrix,) = local_call(
         matrix_kernel, [vmem] * 6, [floats(count, 8 * nodes)], 8 * count * nodes

time: 23.9 us -> 23.9 us (level)
  no operation moved by 1% of the time
where the time goes in v1:
time: 23.9 us; the launch traced here: 23.7 us
  starting transfers between devices  8.37 us (35%)
  Pallas kernels  7.47 us (31%)
  waiting for transfers between devices  4.13 us (17%)
  between operations  2.05 us (9%)
  other arithmetic  1.58 us (7%)
    ppermute x7, starting transfers between devices, across(): return lax.ppermute(array, 'blk', [(i, i ^ mask) for i in range(blk_size)])  8.37 us
    ppermute x7, waiting for transfers between devices, across(): return lax.ppermute(array, 'blk', [(i, i ^ mask) for i in range(blk_size)])  4.13 us
    pallas_call x1, Pallas kernels, doubled_body(): local_call(far_other_kernel, [vmem] * 8, [halves(depth, 2 * nodes), float...  1.81 us
    pallas_call x1, Pallas kernels, doubled_body(): local_call(functools.partial(weight_kernel, assets), [vmem] * 10, [floats...  1.23 us
    pallas_call x1, Pallas kernels, doubled_body(): local_call(functools.partial(far_kernel, sources), [vmem] * 7, [halves(no...  1.15 us
    pallas_call x1, Pallas kernels, doubled_body(): local_call(functools.partial(mid_kernel, sources), [vmem] * 5, [halves(no...  0.88 us
    select_n x1, other arithmetic, doubled_body(): pieces.append(jnp.where(tile_rows < own_slabs, rows, pieces[0]))  0.84 us
    pallas_call x1, Pallas kernels, doubled_body(): local_call(functools.partial(near_kernel, sources), [vmem] * 3, [halves(2...  0.78 us
  transfers between devices with their start and end apart: 7, of which 5 were waited for; matrix products, arithmetic and copies ran while one was open for 3% of the time, Pallas kernels for 19%

profile of v1, /device:TPU:0, one launch (start us, length us, event | category | flops | bytes accessed | tf_op | source)
XLA Modules:
  0.0 23.7 jit_solution(12541359556322390784)
XLA Ops:
  0.6 0.8 %pad_select_fusion = (f32[16,128]{1,0:T(8,128)S(1)}, f32[16,128]{1,0:T(8,128)S(1)}, f32[16,128]{1,0:T(8,128)S(1)}, f32[16,128]{1,0:T(8,128)S(1)}, f32[16,128]{1,0:T(8,128)S(1)}) fusion(f32[2,128]{1,0:T(2,128)} %bitcast.6, pred[16]{0:T(512)(128)(4,1)S(1)} %iota_compare_fusion, f32[16,256]{1,0:T(8,128)} %param.6, f32[16,256]{1,0:T(8,128)} %param.7), kind=kLoop, calls=%fused_computation.3 | loop fusion | flops 2048 | bytes 74768 | tf_op jit(solution)/shard_map/jit(_where)/select_n | solution.py:373
  1.5 4.1 %collective-permute-start = (f32[66,128]{1,0:T(8,128)S(1)}, f32[66,128]{1,0:T(8,128)S(1)}, u32[]{:S(2)}, u32[]{:S(2)}) collective-permute-start(f32[66,128]{1,0:T(8,128)S(1)} %shard_map.77.packed_ref), channel_id=1, source_target_pairs={{0,8},{1,9},{2,10},{3,11},{4,12},{5,13},{6,14},{7,15},{8,0},{9,1},... | collective-permute-start | bytes 101384 | tf_op jit(solution)/shard_map/ppermute | solution.py:356
  6.9 0.7 %pad_maximum_fusion.2.table_ref = f32[13,16]{1,0:T(8,128)S(1)} fusion(f32[1,16]{1,0:T(1,128)S(1)} %compare_select_fusion.1, f32[12,16]{1,0:T(8,128)} %param.9), kind=kLoop, calls=%fused_computation.2 | loop fusion | flops 208 | bytes 1664 | tf_op jit(solution)/shard_map/concatenate | solution.py:379
  7.6 0.1 shard_map.78.columns_ref
  7.8 0.2 collective-permute-done
  8.0 1.6 %collective-permute-start.1 = (f32[132,128]{1,0:T(8,128)S(1)}, f32[132,128]{1,0:T(8,128)S(1)}, u32[]{:S(2)}, u32[]{:S(2)}) collective-permute-start(f32[132,128]{1,0:T(8,128)S(1)} %concatenate.12.first_ref.packed_ref.refs_0_), channel_id=1, source_target_pairs={{0,4},{1,5},{2,6},{3,7},{4,0},{5,1},{6,2},{7,3},{8,12},{9,13},{10,... | collective-permute-start | bytes 202760 | tf_op jit(solution)/shard_map/ppermute | solution.py:356
  9.6 1.6 %collective-permute-start.2 = (f32[132,128]{1,0:T(8,128)S(1)}, f32[132,128]{1,0:T(8,128)S(1)}, u32[]{:S(2)}, u32[]{:S(2)}) collective-permute-start(f32[132,128]{1,0:T(8,128)S(1)} %concatenate.12.first_ref.packed_ref.refs_0_), channel_id=1, source_target_pairs={{0,6},{1,7},{2,4},{3,5},{4,2},{5,3},{6,0},{7,1},{8,14},{9,15},{10,... | collective-permute-start | bytes 202760 | tf_op jit(solution)/shard_map/ppermute | solution.py:356
  11.2 0.3 %collective-permute-start.3 = (f32[132,128]{1,0:T(8,128)S(1)}, f32[132,128]{1,0:T(8,128)S(1)}, u32[]{:S(2)}, u32[]{:S(2)}) collective-permute-start(f32[132,128]{1,0:T(8,128)S(1)} %concatenate.12.first_ref.packed_ref.refs_0_), channel_id=1, source_target_pairs={{0,2},{1,3},{2,0},{3,1},{4,6},{5,7},{6,4},{7,5},{8,10},{9,11},{10,... | collective-permute-start | bytes 202760 | tf_op jit(solution)/shard_map/ppermute | solution.py:356
  11.5 0.1 shard_map.85.refs_6_
  11.6 0.8 %collective-permute-done.1.second_ref.refs_1_ = f32[132,128]{1,0:T(8,128)S(1)} collective-permute-done((f32[132,128]{1,0:T(8,128)S(1)}, f32[132,128]{1,0:T(8,128)S(1)}, u32[]{:S(2)}, u32[]{:S(2)}) %collective-permute-start.1) | collective-permute-done | bytes 67616 | tf_op jit(solution)/shard_map/ppermute | solution.py:356
  12.5 0.1 collective-permute-start.4
  12.5 2.2 %collective-permute-done.2.mid_ref.refs_2_ = f32[132,128]{1,0:T(8,128)S(1)} collective-permute-done((f32[132,128]{1,0:T(8,128)S(1)}, f32[132,128]{1,0:T(8,128)S(1)}, u32[]{:S(2)}, u32[]{:S(2)}) %collective-permute-start.2) | collective-permute-done | bytes 67616 | tf_op jit(solution)/shard_map/ppermute | solution.py:356
  14.8 0.7 %collective-permute-done.3.far_ref.refs_3_ = f32[132,128]{1,0:T(8,128)S(1)} collective-permute-done((f32[132,128]{1,0:T(8,128)S(1)}, f32[132,128]{1,0:T(8,128)S(1)}, u32[]{:S(2)}, u32[]{:S(2)}) %collective-permute-start.3) | collective-permute-done | bytes 67616 | tf_op jit(solution)/shard_map/ppermute | solution.py:356
  15.5 0.1 collective-permute-start.5
  15.6 0.8 %shard_map.79 = (bf16[1024,128]{1,0:T(8,128)(2,1)S(1)}, bf16[128,1024]{1,0:T(8,128)(2,1)S(1)}, f32[8,128]{1,0:T(8,128)S(1)}) custom-call(f32[2,16,128]{2,1,0:T(8,128)S(1)} %shard_map.78.columns_ref, f32[132,128]{1,0:T(8,128)S(1)} %concatenate.12.first_ref.packed_ref.refs_0_, f32[132,128]{1,0:T(8,128)S(1)} %collective-permute-done.1.second_ref.refs_1_), custom_call_target="tpu_custom_call" | custom-call | flops 268435456 | tf_op jit(solution)/shard_map/pallas_call | solution.py:406
  16.4 0.9 %shard_map.80 = (bf16[512,128]{1,0:T(8,128)(2,1)S(1)}, bf16[128,512]{1,0:T(8,128)(2,1)S(1)}, f32[12,128]{1,0:T(8,128)S(1)}) custom-call(f32[2,16,128]{2,1,0:T(8,128)S(1)} %shard_map.78.columns_ref, f32[132,128]{1,0:T(8,128)S(1)} %collective-permute-done.2.mid_ref.refs_2_, bf16[1024,128]{1,0:T(8,128)(2,1)S(1)} %get-tuple-element.21.near_left.left_ref, ...), custom_call_target="tpu_custom_call" | custom-call | flops 335544320 | tf_op jit(solution)/shard_map/pallas_call | solution.py:418
  17.3 1.1 %shard_map.81 = (bf16[512,128]{1,0:T(8,128)(2,1)S(1)}, bf16[128,512]{1,0:T(8,128)(2,1)S(1)}, f32[16,128]{1,0:T(8,128)S(1)}) custom-call(f32[2,16,128]{2,1,0:T(8,128)S(1)} %shard_map.78.columns_ref, f32[132,128]{1,0:T(8,128)S(1)} %collective-permute-done.3.far_ref.refs_3_, bf16[1024,128]{1,0:T(8,128)(2,1)S(1)} %get-tuple-element.21.near_left.left_ref, ...), custom_call_target="tpu_custom_call" | custom-call | flops 469762048 | tf_op jit(solution)/shard_map/pallas_call | solution.py:425
  18.5 0.0 collective-permute-done.4.other_ref.refs_4_
  18.5 0.7 %shard_map.82 = (bf16[128,1024]{1,0:T(8,128)(2,1)S(1)}, f32[8,128]{1,0:T(8,128)S(1)}) custom-call(f32[2,16,128]{2,1,0:T(8,128)S(1)} %shard_map.78.columns_ref, f32[136,128]{1,0:T(8,128)S(1)} %collective-permute-done.4.other_ref.refs_4_, bf16[1024,128]{1,0:T(8,128)(2,1)S(1)} %get-tuple-element.21.near_left.left_ref), custom_call_target="tpu_custom_call" | custom-call | flops 268435456 | tf_op jit(solution)/shard_map/pallas_call | solution.py:412
  19.2 0.0 collective-permute-done.5.other_ref.refs_5_
  19.2 1.8 %shard_map.83 = (bf16[128,1024]{1,0:T(8,128)(2,1)S(1)}, f32[32,128]{1,0:T(8,128)S(1)}) custom-call(f32[2,16,128]{2,1,0:T(8,128)S(1)} %shard_map.78.columns_ref, f32[136,128]{1,0:T(8,128)S(1)} %collective-permute-done.5.other_ref.refs_5_, bf16[1024,128]{1,0:T(8,128)(2,1)S(1)} %get-tuple-element.21.near_left.left_ref, ...), custom_call_target="tpu_custom_call" | custom-call | flops 805306368 | tf_op jit(solution)/shard_map/pallas_call | solution.py:431
  21.0 0.6 %collective-permute-start.6 = (f32[32,128]{1,0:T(8,128)S(1)}, f32[32,128]{1,0:T(8,128)S(1)}, u32[]{:S(2)}, u32[]{:S(2)}) collective-permute-start(f32[32,128]{1,0:T(8,128)S(1)} %get-tuple-element.33.density_ref), channel_id=1, source_target_pairs={{0,1},{1,0},{2,3},{3,2},{4,5},{5,4},{6,7},{7,6},{8,9},{9,8},{10,11... | collective-permute-start | bytes 49160 | tf_op jit(solution)/shard_map/ppermute | solution.py:356
  21.6 0.7 %shard_map.84.matrix_ref = f32[256,4096]{1,0:T(8,128)S(1)} custom-call(bf16[256,128]{1,0:T(8,128)(2,1)S(1)} %slice.67.left_ref, bf16[128,1024]{1,0:T(8,128)(2,1)S(1)} %get-tuple-element.22.near_right.refs_0_, bf16[128,512]{1,0:T(8,128)(2,1)S(1)} %get-tuple-element.24.mid_right.refs_1_, bf16[128,512]{1,0:T(8,128)(2,1)S(1)} %get-tuple-element.27.refs_2_, ...), custom_call_target="tpu_custom_call" | custom-call | flops 268435456 | tf_op jit(solution)/shard_map/pallas_call | solution.py:438
  22.3 0.1 collective-permute-done.6.received_ref
  22.4 1.2 %shard_map.86 = (f32[2,128]{1,0:T(2,128)}, f32[2,128]{1,0:T(2,128)}) custom-call(f32[256,4096]{1,0:T(8,128)S(1)} %shard_map.84.matrix_ref, f32[32,128]{1,0:T(8,128)S(1)} %get-tuple-element.33.density_ref, f32[32,128]{1,0:T(8,128)S(1)} %collective-permute-done.6.received_ref, f32[132,128]{1,0:T(8,128)S(1)} %concatenate.12.first_ref.packed_ref.refs_0_, ...), custom_call_target="tpu_custom_call" | custom-call | tf_op jit(solution)/shard_map/pallas_call | solution.py:441
  (19 shorter events, 0.1 us)
Async XLA Ops:
  1.5 6.5 %collective-permute-start = (f32[66,128]{1,0:T(8,128)S(1)}, f32[66,128]{1,0:T(8,128)S(1)}, u32[]{:S(2)}, u32[]{:S(2)}) collective-permute-start(f32[66,128]{1,0:T(8,128)S(1)} %shard_map.77.packed_ref), channel_id=1, source_target_pairs={{0,8},{1,9},{2,10},{3,11},{4,12},{5,13},{6,14},{7,15},{8,0},{9,1},... | collective-permute-start | bytes 101384 | tf_op jit(solution)/shard_map/ppermute | solution.py:356
  8.0 4.5 %collective-permute-start.1 = (f32[132,128]{1,0:T(8,128)S(1)}, f32[132,128]{1,0:T(8,128)S(1)}, u32[]{:S(2)}, u32[]{:S(2)}) collective-permute-start(f32[132,128]{1,0:T(8,128)S(1)} %concatenate.12.first_ref.packed_ref.refs_0_), channel_id=1, source_target_pairs={{0,4},{1,5},{2,6},{3,7},{4,0},{5,1},{6,2},{7,3},{8,12},{9,13},{10,... | collective-permute-start | bytes 202760 | tf_op jit(solution)/shard_map/ppermute | solution.py:356
  9.6 5.2 %collective-permute-start.2 = (f32[132,128]{1,0:T(8,128)S(1)}, f32[132,128]{1,0:T(8,128)S(1)}, u32[]{:S(2)}, u32[]{:S(2)}) collective-permute-start(f32[132,128]{1,0:T(8,128)S(1)} %concatenate.12.first_ref.packed_ref.refs_0_), channel_id=1, source_target_pairs={{0,6},{1,7},{2,4},{3,5},{4,2},{5,3},{6,0},{7,1},{8,14},{9,15},{10,... | collective-permute-start | bytes 202760 | tf_op jit(solution)/shard_map/ppermute | solution.py:356
  11.2 4.3 %collective-permute-start.3 = (f32[132,128]{1,0:T(8,128)S(1)}, f32[132,128]{1,0:T(8,128)S(1)}, u32[]{:S(2)}, u32[]{:S(2)}) collective-permute-start(f32[132,128]{1,0:T(8,128)S(1)} %concatenate.12.first_ref.packed_ref.refs_0_), channel_id=1, source_target_pairs={{0,2},{1,3},{2,0},{3,1},{4,6},{5,7},{6,4},{7,5},{8,10},{9,11},{10,... | collective-permute-start | bytes 202760 | tf_op jit(solution)/shard_map/ppermute | solution.py:356
  12.5 6.0 %collective-permute-start.4 = (f32[136,128]{1,0:T(8,128)S(1)}, f32[136,128]{1,0:T(8,128)S(1)}, u32[]{:S(2)}, u32[]{:S(2)}) collective-permute-start(f32[136,128]{1,0:T(8,128)S(1)} %pad_maximum_fusion), channel_id=1, source_target_pairs={{0,1},{1,0},{2,3},{3,2},{4,5},{5,4},{6,7},{7,6},{8,9},{9,8},{10,11... | collective-permute-start | bytes 208904 | tf_op jit(solution)/shard_map/ppermute | solution.py:356
  15.5 3.7 %collective-permute-start.5 = (f32[136,128]{1,0:T(8,128)S(1)}, f32[136,128]{1,0:T(8,128)S(1)}, u32[]{:S(2)}, u32[]{:S(2)}) collective-permute-start(f32[136,128]{1,0:T(8,128)S(1)} %pad_maximum_fusion.1), channel_id=1, source_target_pairs={{0,1},{1,0},{2,3},{3,2},{4,5},{5,4},{6,7},{7,6},{8,9},{9,8},{10,11... | collective-permute-start | bytes 208904 | tf_op jit(solution)/shard_map/ppermute | solution.py:356
  21.0 1.4 %collective-permute-start.6 = (f32[32,128]{1,0:T(8,128)S(1)}, f32[32,128]{1,0:T(8,128)S(1)}, u32[]{:S(2)}, u32[]{:S(2)}) collective-permute-start(f32[32,128]{1,0:T(8,128)S(1)} %get-tuple-element.33.density_ref), channel_id=1, source_target_pairs={{0,1},{1,0},{2,3},{3,2},{4,5},{5,4},{6,7},{7,6},{8,9},{9,8},{10,11... | collective-permute-start | bytes 49160 | tf_op jit(solution)/shard_map/ppermute | solution.py:356
